TPU v7x, 32 devices: a whole 2x2x4 slice. The times are simulated.
32 devices in a mesh: grp: 4 (over z), freq: 8 (over y, x, core).
Axes of the slice: x: 2, y: 2, z: 4, core: 2. Of those that a mesh axis runs over, the one named last changes fastest.
Arguments:
- sources: bfloat16 [1024, 32768], P('freq', 'grp'), may hold values from -6 to 6
- panel_pos: float32 [3, 32768], P(None, 'grp'), may hold values from -1 to 1
- panel_blade: int32 [32768], P('grp'), may hold values from 0 to 3
- observer_table: float32 [3, 2048], replicated, may hold values from -8 to 8, as said below
- observer_index: int32 [32], replicated, may hold values from 0 to 2047
Outputs:
- spectra: float32 [512, 4, 2, 32], P('freq', 'grp')
Inputs may be any that keep to these rules, and one draw needn't show every extreme that they name: `observer_table`: each observer lies 3 to 8 units from the anchor (0, 0, 0).
All inputs are finite; a program needn't handle non-finite values.
Results may differ from a plain program's by a relative error of at most 0.0047.
Values may be sent and summed in bfloat16 or wider, within the bound.
A program may use at most 64 MiB of HBM per device.

v0:
```python
import math

import jax
import jax.numpy as jnp
from jax import lax
from jax.sharding import PartitionSpec as P

NT = 1024
NF = 512
NCOMP = 4


wave_step = 0.04


def transform_table():
    row_index = jnp.arange(2 * NF, dtype=jnp.int32)
    samples = jnp.arange(NT, dtype=jnp.int32)
    frequency = row_index // 2
    parity = row_index % 2
    turn_count = frequency[:, None] * samples[None, :] % NT
    angle_table = 2.0 * math.pi / NT * turn_count.astype(jnp.float32)
    values = jnp.where(parity[:, None] == 0, jnp.cos(angle_table), -jnp.sin(angle_table))
    return (values / math.sqrt(NT)).astype(jnp.bfloat16)


def distances(positions, observers):
    offset_x = observers[0][:, None] - positions[0][None, :]
    offset_y = observers[1][:, None] - positions[1][None, :]
    offset_z = observers[2][:, None] - positions[2][None, :]
    return jnp.sqrt(offset_x * offset_x + offset_y * offset_y + offset_z * offset_z)


def blade_masks(blades):
    return (blades[None, :] == jnp.arange(NCOMP, dtype=jnp.int32)[:, None]).astype(jnp.bfloat16)


def frequency_term(frequency, spectrum_pair, blade_mask, distance, amplitude):
    wavenumber = wave_step * frequency.astype(jnp.float32)
    phase_angle = wavenumber * distance
    green_matrix = jnp.concatenate(
        [jnp.cos(phase_angle) * amplitude, -jnp.sin(phase_angle) * amplitude], axis=0
    ).astype(jnp.bfloat16)
    weighted = jnp.concatenate(
        [spectrum_pair[0][None, :] * blade_mask, spectrum_pair[1][None, :] * blade_mask], axis=0
    )
    product = lax.dot_general(
        weighted, green_matrix, (((1,), (1,)), ((), ())), preferred_element_type=jnp.float32
    )
    blade_count = blade_mask.shape[0]
    observer_count = distance.shape[0]
    real_part = product[:blade_count, :observer_count] - product[blade_count:, observer_count:]
    imag_part = product[:blade_count, observer_count:] + product[blade_count:, :observer_count]
    return jnp.stack([real_part, imag_part], axis=1)


def body(sources, panel_pos, panel_blade, observer_table, observer_index):
    freq_share = NF // lax.axis_size("freq")
    position = lax.axis_index("freq")
    observers = observer_table[:, observer_index]
    dft_table = transform_table()
    device_count = lax.axis_size("freq")
    shaped = sources.reshape(sources.shape[0], device_count, sources.shape[1] // device_count)
    piece = lax.all_to_all(shaped, "freq", split_axis=1, concat_axis=0, tiled=True)
    item_count = piece.shape[2]
    flat = piece.reshape(piece.shape[0], item_count)
    local_spec = jnp.dot(dft_table, flat, preferred_element_type=jnp.float32).astype(jnp.bfloat16)
    gathered = lax.all_to_all(
        local_spec.reshape(2 * NF, 1, item_count), "freq", split_axis=0, concat_axis=1, tiled=True
    )
    received = gathered.reshape(gathered.shape[0], gathered.shape[1] * gathered.shape[2])
    spectra_pairs = received.reshape(freq_share, 2, received.shape[1])
    distance = distances(panel_pos, observers)
    amplitude = 0.25 / (math.pi * distance)
    blade_mask = blade_masks(panel_blade)
    frequencies = position * freq_share + jnp.arange(freq_share, dtype=jnp.int32)

    def per_frequency(element):
        return frequency_term(element[0], element[1], blade_mask, distance, amplitude)

    partial_value = lax.map(per_frequency, (frequencies, spectra_pairs))
    summed = lax.psum(partial_value, "grp")
    blade_share = NCOMP // lax.axis_size("grp")
    return lax.dynamic_slice_in_dim(summed, lax.axis_index("grp") * blade_share, blade_share, 1)


def solution(mesh):
    in_specs = (P("freq", "grp"), P(None, "grp"), P("grp"), P(), P())
    out_specs = P("freq", "grp", None, None)
    return jax.shard_map(body, mesh=mesh, in_specs=in_specs, out_specs=out_specs, check_vma=False)
```

profile of v0, /device:TPU:0, one launch (start us, length us, event | category | flops | bytes accessed | tf_op | source)
XLA Modules:
  0.0 632.9 jit_solution(9008926720111402404)
XLA Ops:
  10.6 5.2 all-to-all-start
  17.1 25.4 %all-to-all-done = bf16[128,8,1024]{0,2,1:T(8,128)(2,1)S(1)} async-done(((bf16[128,8,1024]{0,2,1:T(8,128)(2,1)}), bf16[128,8,1024]{0,2,1:T(8,128)(2,1)S(1)}, u32[]{:S(2)}, u32[]{:S(2)}) %all-to-all-start) | async-done | bytes 2097184 | tf_op jit(solution)/shard_map/all_to_all | solution.py:64
  45.1 22.1 %convert_bitcast_fusion = bf16[1024,1,1024]{2,0,1:T(8,128)(2,1)} fusion(bf16[1024,1024]{1,0:T(8,128)(2,1)} %bitcast.37, s32[1024]{0:T(1024)S(1)} %add_select_fusion.1, pred[1024]{0:T(1024)(128)(4,1)S(1)} %fusion.32), kind=kOutput, calls=%fused_computation.37 | convolution fusion | flops 2167406592 | bytes 4199424 | tf_op jit(solution)/shard_map/dot_general | solution.py:67
  79.4 26.2 %all-to-all-done.1 = bf16[8,2,65536]{2,1,0:T(2,128)(2,1)S(1)} async-done(((bf16[8,2,65536]{2,1,0:T(2,128)(2,1)}), bf16[8,2,65536]{2,1,0:T(2,128)(2,1)S(1)}, u32[]{:S(2)}, u32[]{:S(2)}) %all-to-all-start.1) | async-done | bytes 2097184 | tf_op jit(solution)/shard_map/all_to_all | solution.py:68
  117.0 472.7 %while.12 = (s32[]{:T(128)}, f32[64,4,2,32]{3,1,2,0:T(4,128)S(1)}, bf16[64,2,8192]{2,1,0:T(2,128)(2,1)}, s32[64]{0:T(128)S(1)}, s32[8192]{0:T(1024)S(1)}, /*inde...) while((s32[]{:T(128)}, f32[64,4,2,32]{3,1,2,0:T(4,128)S(1)}, ...), condition=%wide.region_1.2_spmd.clone.clone, body=%wide.region_0.1_spmd.clone.clone.sunk | while | flops 15041029 | bytes 2602569 | solution.py:81
  118.2 4.6 multiply_convert_fusion.7
  147.7 4.6 multiply_convert_fusion.7
  155.1 4.6 multiply_convert_fusion.7
  177.3 4.6 multiply_convert_fusion.7
  184.7 4.6 multiply_convert_fusion.7
  214.2 4.6 multiply_convert_fusion.7
  221.6 4.6 multiply_convert_fusion.7
  251.1 4.6 multiply_convert_fusion.7
  258.5 4.6 multiply_convert_fusion.7
  288.1 4.6 multiply_convert_fusion.7
  295.4 4.6 multiply_convert_fusion.7
  317.6 4.6 multiply_convert_fusion.7
  325.0 4.6 multiply_convert_fusion.7
  354.5 4.6 multiply_convert_fusion.7
  361.9 4.6 multiply_convert_fusion.7
  391.5 4.6 multiply_convert_fusion.7
  398.9 4.6 multiply_convert_fusion.7
  428.4 4.6 multiply_convert_fusion.7
  435.8 4.6 multiply_convert_fusion.7
  457.9 4.6 multiply_convert_fusion.7
  465.3 4.6 multiply_convert_fusion.7
  494.9 4.6 multiply_convert_fusion.7
  502.3 4.6 multiply_convert_fusion.7
  531.8 4.6 multiply_convert_fusion.7
  539.2 4.6 multiply_convert_fusion.7
  568.7 4.6 multiply_convert_fusion.7
  590.5 34.2 %all-reduce.2.cloned.1.call-done = f32[64,4,2,32]{0,3,2,1:T(8,128)} async-done(((f32[64,4,2,32]{0,3,2,1:T(8,128)}), f32[64,4,2,32]{0,3,2,1:T(8,128)}) %all-reduce.2.cloned.1.call-update) | async-done | bytes 65552 | tf_op jit(solution)/shard_map/psum | solution.py:82
  (454 shorter events, 345.9 us)
Async XLA Ops:
  6.5 9.3 %copy-start.2 = (f32[3,2048]{1,0:T(4,128)S(1)}, f32[3,2048]{1,0:T(4,128)}, u32[]{:S(2)}) copy-start(f32[3,2048]{1,0:T(4,128)} %param.10) | copy-start | bytes 73732
  6.5 9.7 %copy-start.3 = (s32[32]{0:T(128)S(1)}, s32[32]{0:T(128)}, u32[]{:S(2)}) copy-start(s32[32]{0:T(128)} %param.11) | copy-start | bytes 388
  10.6 31.8 %all-to-all-start = ((bf16[128,8,1024]{0,2,1:T(8,128)(2,1)}), bf16[128,8,1024]{0,2,1:T(8,128)(2,1)S(1)}, u32[]{:S(2)}, u32[]{:S(2)}) async-start(bf16[128,8,1024]{0,2,1:T(8,128)(2,1)} %bitcast.36), calls=%async_computation | async-start | bytes 4194304 | tf_op jit(solution)/shard_map/all_to_all | solution.py:64
  71.6 7.7 %copy-start.1 = (f32[3,8192]{1,0:T(4,128)S(1)}, f32[3,8192]{1,0:T(4,128)}, u32[]{:S(2)}) copy-start(f32[3,8192]{1,0:T(4,128)} %param.8) | copy-start | bytes 294916
  75.4 30.2 %all-to-all-start.1 = ((bf16[8,2,65536]{2,1,0:T(2,128)(2,1)}), bf16[8,2,65536]{2,1,0:T(2,128)(2,1)S(1)}, u32[]{:S(2)}, u32[]{:S(2)}) async-start(bf16[8,2,65536]{2,1,0:T(2,128)(2,1)} %reshape.63), calls=%async_computation.1 | async-start | bytes 4194304 | tf_op jit(solution)/shard_map/all_to_all | solution.py:68
  79.1 545.6 %all-reduce.2.cloned.1.call-start = ((), (), s32[]{:S(2)}) async-start(), calls=%async_computation.2 | async-start | bytes 262144 | tf_op jit(solution)/shard_map/psum | solution.py:82
  113.0 4.0 copy-start
Sparse Core Ops, SparseCore 0:
  590.6 34.0 all-reduce.1
where the time goes:
time: 639 us; the launch traced here: 633 us
  other arithmetic  307 us (48%)
  local copies, waits for them, and re-layouts  130 us (20%)
  waiting for transfers between devices  85.8 us (13%)
  matrix products  46 us (7%)
  loops' own time  41.1 us (6%)
  between operations  13.5 us (2%)
  starting transfers between devices  9.02 us (1%)
    another operation x64, other arithmetic  294 us
    slice x64, local copies, waits for them, and re-layouts, frequency_term(): spectrum_pair[0][None, :] * blade_mask  65.3 us
    another operation x1, loops' own time, body(): partial_value = lax.map(per_frequency, (frequencies, spectra_pairs))  41.1 us
    dynamic_slice x64, local copies, waits for them, and re-layouts, body(): partial_value = lax.map(per_frequency, (frequencies, spectra_pairs))  38.9 us
    psum x1, waiting for transfers between devices, body(): summed = lax.psum(partial_value, 'grp')  34.2 us
    all_to_all x1, waiting for transfers between devices, body(): lax.all_to_all(local_spec.reshape(2 * NF, 1, item_count), 'freq', split_a...  26.2 us
    all_to_all x1, waiting for transfers between devices, body(): lax.all_to_all(shaped, 'freq', split_axis=1, concat_axis=0, tiled=True)  25.4 us
    dot_general x64, matrix products, frequency_term(): lax.dot_general(weighted, green_matrix, (((1,), (1,)), ((), ())), preferr...  23.9 us
  transfers between devices with their start and end apart: 3, of which 3 were waited for; matrix products, arithmetic and copies ran while one was open for 0% of the time, Pallas kernels for 0%

commit v1 on v0

v1 whole, which is shorter than its diff:
```python
import functools
import math

import jax
import jax.numpy as jnp
import numpy as np
from jax import lax
from jax.experimental import pallas as pl
from jax.experimental.pallas import tpu as pltpu
from jax.sharding import PartitionSpec as P

NT = 1024
NF = 512
NCOMP = 4
WAVE_STEP = 0.04
LANES = 128
CHUNK = 256
STEPS = 8


def transform_table():
    turns = (np.arange(NF)[:, None] * np.arange(NT)[None, :]) % NT
    angle = 2.0 * math.pi / NT * turns
    values = np.stack([np.cos(angle), -np.sin(angle)], axis=1).reshape(2 * NF, NT)
    return jnp.asarray((values / math.sqrt(NT)).astype(np.float32)).astype(jnp.bfloat16)


def cos_sin(x):
    y = x * x
    cos = jnp.full_like(y, 1.0 / math.factorial(16))
    sin = jnp.full_like(y, -1.0 / math.factorial(15))
    for n in range(7, -1, -1):
        sign = 1.0 if n % 2 == 0 else -1.0
        cos = cos * y + sign / math.factorial(2 * n)
        if n < 7:
            sin = sin * y + sign / math.factorial(2 * n + 1)
    return cos, sin * x


def start_states(pos_ref, obs_ref, states, row0, share):
    rows = 32
    lane = lax.broadcasted_iota(jnp.int32, (rows, LANES), 1)
    j = (lane // (LANES // share)).astype(jnp.float32)
    for r in range(CHUNK // rows):
        at = pl.ds(row0 + r * rows, rows)
        d2 = None
        for axis in range(3):
            diff = obs_ref[axis : axis + 1, :] - pos_ref[at, axis : axis + 1]
            d2 = diff * diff if d2 is None else d2 + diff * diff
        d = jnp.sqrt(d2)
        amplitude = 0.25 / (math.pi * d)
        theta = WAVE_STEP * d
        cj, sj = cos_sin(j * theta)
        cs, ss = cos_sin(float(share) * theta)
        cj, sj = cj * amplitude, sj * amplitude
        out = pl.ds(r * rows, rows)
        states[0, out, :] = cj * cs + sj * ss
        states[1, out, :] = cj
        states[2, out, :] = sj * cs - cj * ss
        states[3, out, :] = sj
        states[4, out, :] = 2.0 * cs


def green_rows(states, green, r):
    at = pl.ds(r * 16, 16)
    c0, c1, s0, s1, t = (states[i, at, :] for i in range(5))
    for k in range(STEPS):
        green[k, at, :LANES] = c1.astype(jnp.bfloat16)
        green[k, at, LANES:] = s1.astype(jnp.bfloat16)
        c0, c1 = c1, t * c1 - c0
        s0, s1 = s1, t * s1 - s0
    states[0, at, :], states[1, at, :] = c0, c1
    states[2, at, :], states[3, at, :] = s0, s1


def contract(spec, mask, green, acc, step, k, share, first):
    sub = lax.broadcasted_iota(jnp.int32, (2 * NCOMP, CHUNK), 0)
    real_row = sub < NCOMP
    rows = []
    base = pl.multiple_of(step * 2 * share, 2 * share)
    pair = spec[pl.ds(base, 2 * share), :]
    for j in range(share):
        re = jnp.broadcast_to(pair[2 * j : 2 * j + 1, :], (2 * NCOMP, CHUNK))
        im = jnp.broadcast_to(pair[2 * j + 1 : 2 * j + 2, :], (2 * NCOMP, CHUNK))
        rows.append(jnp.where(real_row, re, im) * mask)
    weighted = jnp.concatenate(rows, axis=0).astype(jnp.bfloat16)
    prod = jnp.dot(weighted, green[k], preferred_element_type=jnp.float32)
    lane = lax.broadcasted_iota(jnp.int32, (2 * NCOMP, LANES), 1) // (LANES // share)
    even = prod[: 2 * NCOMP, :LANES]
    odd = prod[: 2 * NCOMP, LANES:]
    for j in range(1, share):
        block = prod[2 * NCOMP * j : 2 * NCOMP * (j + 1)]
        even = jnp.where(lane == j, block[:, :LANES], even)
        odd = jnp.where(lane == j, block[:, LANES:], odd)
    odd = jnp.concatenate([odd[NCOMP:], -odd[:NCOMP]], axis=0)
    total = even + odd
    if first:
        acc[step] = total
    else:
        acc[step] = acc[step] + total


def block_pair(spec, mask, now, acc, block, share, first, states, later):
    per = CHUNK // 16 // STEPS
    for k in range(STEPS):
        if now is not None:
            contract(spec, mask, now, acc, block * STEPS + k, k, share, first)
        if later is not None:
            for r in range(per):
                green_rows(states, later, k * per + r)


def phase(q, first, table_ref, block_of, pos_ref, blade_ref, obs_ref, acc, spec, states, mask, ga, gb, share):
    row0 = pl.multiple_of(q * CHUNK, CHUNK)
    start_states(pos_ref, obs_ref, states, row0, share)
    sub = lax.broadcasted_iota(jnp.int32, (2 * NCOMP, CHUNK), 0) % NCOMP
    mask[...] = jnp.where(blade_ref[:, pl.ds(row0, CHUNK)] == sub, 1.0, 0.0)
    block_pair(None, None, None, None, 0, share, first, states, ga)
    data = block_of(q)
    for r in range(4):
        part = pl.ds(r * (2 * NF // 4), 2 * NF // 4)
        spec[part, :] = (
            jnp.dot(table_ref[part, :], data, preferred_element_type=jnp.float32)
            .astype(jnp.bfloat16)
            .astype(jnp.float32)
        )
    blocks = NF // share // STEPS
    m = mask[...]

    def two(i, carry):
        block_pair(spec, m, ga, acc, 2 * i, share, first, states, gb)
        block_pair(spec, m, gb, acc, 2 * i + 1, share, first, states, ga)
        return carry

    lax.fori_loop(0, blocks // 2, two, 0)


def kernel(share, table_ref, data_ref, pos_ref, blade_ref, obs_ref, acc, spec, states, mask, ga, gb):
    def block_of(q):
        return data_ref[:, pl.ds(pl.multiple_of(q * CHUNK, CHUNK), CHUNK)]

    acc[...] = jnp.zeros_like(acc)

    def step(q, carry):
        phase(q, False, table_ref, block_of, pos_ref, blade_ref, obs_ref, acc, spec, states, mask, ga, gb, share)
        return carry

    lax.fori_loop(0, data_ref.shape[1] // CHUNK, step, 0)


def body(sources, panel_pos, panel_blade, observer_table, observer_index):
    nfreq, ngrp = lax.axis_size("freq"), lax.axis_size("grp")
    me = lax.axis_index("freq")
    nobs = observer_index.shape[0]
    share = LANES // nobs
    panels = sources.shape[1] // nfreq
    observers = jnp.tile(observer_table[:, observer_index], (1, share))
    pos = lax.dynamic_slice_in_dim(panel_pos, me * panels, panels, 1).T
    blade = lax.dynamic_slice_in_dim(panel_blade, me * panels, panels, 0)[None, :]
    shaped = sources.reshape(sources.shape[0], nfreq, panels)
    piece = lax.all_to_all(shaped, "freq", split_axis=1, concat_axis=0, tiled=True).reshape(NT, panels)
    steps = NF // share
    partial = pl.pallas_call(
        functools.partial(kernel, share),
        out_shape=jax.ShapeDtypeStruct((steps, 2 * NCOMP, LANES), jnp.float32),
        in_specs=[pl.BlockSpec(memory_space=pltpu.VMEM)] * 5,
        out_specs=pl.BlockSpec(memory_space=pltpu.VMEM),
        scratch_shapes=[
            pltpu.VMEM((2 * NF, CHUNK), jnp.float32),
            pltpu.VMEM((5, CHUNK, LANES), jnp.float32),
            pltpu.VMEM((2 * NCOMP, CHUNK), jnp.float32),
            pltpu.VMEM((STEPS, CHUNK, 2 * LANES), jnp.bfloat16),
            pltpu.VMEM((STEPS, CHUNK, 2 * LANES), jnp.bfloat16),
        ],
    )(transform_table(), piece, pos, blade, observers)
    mine = steps // nfreq
    parts = lax.all_to_all(partial.reshape(nfreq, mine, 2 * NCOMP, LANES), "freq", split_axis=0, concat_axis=0, tiled=True)
    summed = jnp.sum(parts, axis=0)
    blades = summed.reshape(mine, 2, ngrp, NCOMP // ngrp, LANES).transpose(2, 0, 1, 3, 4)
    got = jnp.sum(lax.all_to_all(blades, "grp", split_axis=0, concat_axis=0, tiled=True), axis=0)
    got = got.reshape(mine, 2, NCOMP // ngrp, share, nobs).transpose(0, 3, 2, 1, 4)
    return got.reshape(mine * share, NCOMP // ngrp, 2, nobs)


def solution(mesh):
    in_specs = (P("freq", "grp"), P(None, "grp"), P("grp"), P(), P())
    out_specs = P("freq", "grp", None, None)
    return jax.shard_map(body, mesh=mesh, in_specs=in_specs, out_specs=out_specs, check_vma=False)
```

time: 639 us -> 93.8 us (0.15)
  other arithmetic: 307 us -> 0.07 us
  local copies, waits for them, and re-layouts: 130 us -> 9.43 us
  waiting for transfers between devices: 85.8 us -> 22.5 us
  matrix products: 46 us -> 0 us
  loops' own time: 41.1 us -> 0 us
  Pallas kernels: 0 us -> 32.3 us
  blocking collectives: 0 us -> 23.5 us
  between operations: 13.5 us -> 0.09 us
    another operation x128 -> x0, other arithmetic: 298 us -> none
    slice x66 -> x0, local copies, waits for them, and re-layouts: 65.6 us -> none  [the longest x64 65.3 us: frequency_term(): spectrum_pair[0][None, :] * blade_mask]
    dot_general x65 -> x0, matrix products: 46 us -> none  [the longest x64 23.9 us: frequency_term(): lax.dot_general(weighted, green_matrix, (((1,), (1,)), ((), ())), preferr...]
    another operation x1 -> x0, loops' own time: 41.1 us -> none  [body(): partial_value = lax.map(per_frequency, (frequencies, spectra_pairs))]
    dynamic_slice x65 -> x2, local copies, waits for them, and re-layouts: 40.3 us -> 1.29 us  [the longest x1 1.28 us: body(): lax.dynamic_slice_in_dim(panel_blade, me * panels, panels, 0)[None, :]]
    psum x1 -> x0, waiting for transfers between devices: 34.2 us -> none  [body(): summed = lax.psum(partial_value, 'grp')]
    pallas_call x0 -> x1, Pallas kernels: none -> 32.3 us  [body(): pl.pallas_call(functools.partial(kernel, share), out_shape=jax.ShapeDtype...]
    all_to_all x1 -> x0, waiting for transfers between devices: 26.2 us -> none  [body(): lax.all_to_all(local_spec.reshape(2 * NF, 1, item_count), 'freq', split_a...]
  transfers between devices with their start and end apart: 3 -> 1, of which waited for: 3 -> 1; matrix products, arithmetic and copies ran while one was open for 0% -> 4% of each run, Pallas kernels for 0% -> 0%
where the time goes in v1:
time: 93.8 us; the launch traced here: 93.3 us
  Pallas kernels  32.3 us (34%)
  blocking collectives  23.5 us (25%)
  waiting for transfers between devices  22.5 us (24%)
  local copies, waits for them, and re-layouts  9.43 us (10%)
  starting transfers between devices  5.33 us (6%)
    pallas_call x1, Pallas kernels, body(): pl.pallas_call(functools.partial(kernel, share), out_shape=jax.ShapeDtype...  32.3 us
    all_to_all x1, waiting for transfers between devices, body(): lax.all_to_all(shaped, 'freq', split_axis=1, concat_axis=0, tiled=True)  22.5 us
    all_to_all x1, blocking collectives, body(): lax.all_to_all(partial.reshape(nfreq, mine, 2 * NCOMP, LANES), 'freq', sp...  13.1 us
    all_to_all x1, blocking collectives, body(): lax.all_to_all(blades, 'grp', split_axis=0, concat_axis=0, tiled=True)  10.4 us
    all_to_all x1, starting transfers between devices, body(): lax.all_to_all(shaped, 'freq', split_axis=1, concat_axis=0, tiled=True)  5.33 us
    reshape x1, local copies, waits for them, and re-layouts, body(): shaped = sources.reshape(sources.shape[0], nfreq, panels)  3.21 us
    unnamed x10, local copies, waits for them, and re-layouts  2.75 us
  transfers between devices with their start and end apart: 1, of which 1 were waited for; matrix products, arithmetic and copies ran while one was open for 4% of the time, Pallas kernels for 0%

profile of v1, /device:TPU:0, one launch (start us, length us, event | category | flops | bytes accessed | tf_op | source)
XLA Modules:
  0.0 93.3 jit_solution(1231609169847726889)
XLA Ops:
  0.0 0.0 copy-start
  0.0 3.2 %copy.38 = bf16[16,8,8,1024]{3,2,0,1:T(8,128)(2,1)} copy(bf16[16,8,8,1024]{3,2,1,0:T(8,128)(2,1)} %bitcast.23) | data formatting | bytes 4194304 | tf_op jit(solution)/shard_map/reshape | solution.py:160
  3.2 0.0 copy-start.2
  3.2 0.0 copy-start.3
  3.2 5.3 %all-to-all-start = ((bf16[128,8,1024]{2,0,1:T(8,128)(2,1)}), bf16[128,8,1024]{2,0,1:T(8,128)(2,1)S(1)}, u32[]{:S(2)}, u32[]{:S(2)}) async-start(bf16[128,8,1024]{2,0,1:T(8,128)(2,1)} %bitcast.22), calls=%async_computation | async-start | bytes 4194304 | tf_op jit(solution)/shard_map/all_to_all | solution.py:161
  8.6 0.0 copy-done
  8.6 1.0 %copy.35 = f32[3,1024]{0,1:T(8,128)} copy(f32[3,1024]{1,0:T(4,128)S(1)} %constant_dynamic-slice_fusion) | data formatting | bytes 24576
  9.6 1.3 %dynamic_slice.7 = s32[1024]{0:T(1024)} dynamic-slice(s32[8192]{0:T(1024)} %param.8, s32[]{:T(128)S(6)} %select_n.7), dynamic_slice_sizes={1024} | dynamic-slice | bytes 8196 | tf_op jit(solution)/shard_map/dynamic_slice | solution.py:159
  10.9 0.0 copy-done.2
  10.9 0.4 copy.29
  11.3 0.0 copy-done.3
  11.3 0.6 gather_fusion
  11.9 0.1 copy.30
  11.9 0.7 tile.10.obs_ref
  12.6 22.5 %all-to-all-done = bf16[128,8,1024]{2,0,1:T(8,128)(2,1)S(1)} async-done(((bf16[128,8,1024]{2,0,1:T(8,128)(2,1)}), bf16[128,8,1024]{2,0,1:T(8,128)(2,1)S(1)}, u32[]{:S(2)}, u32[]{:S(2)}) %all-to-all-start) | async-done | bytes 2097184 | tf_op jit(solution)/shard_map/all_to_all | solution.py:161
  35.2 0.0 copy-start.1
  35.2 1.3 %copy-done.1 = bf16[128,8,1024]{2,0,1:T(8,128)(2,1)} copy-done((bf16[128,8,1024]{2,0,1:T(8,128)(2,1)}, bf16[128,8,1024]{2,0,1:T(8,128)(2,1)S(1)}, u32[]{:S(2)}) %copy-start.1) | copy-done | bytes 2097176
  36.5 32.3 %shard_map.64 = f32[128,8,128]{2,1,0:T(8,128)} custom-call(bf16[1024,1024]{1,0:T(8,128)(2,1)} %constant.18.table_ref, bf16[1024,1024]{1,0:T(8,128)(2,1)} %bitcast.21, f32[1024,3]{1,0:T(8,128)} %bitcast.24, s32[1,1024]{1,0:T(1,128)} %bitcast.29, f32[3,128]{1,0:T(4,128)} %tile.10.obs_ref), custom_call_target="tpu_custom_call" | custom-call | tf_op jit(solution)/shard_map/pallas_call | solution.py:163
  68.9 13.1 %all_to_all.25 = f32[8,16,8,128]{3,2,1,0:T(8,128)S(1)} all-to-all(f32[8,16,8,128]{3,2,1,0:T(8,128)} %bitcast.25), channel_id=1, replica_groups=mesh['grp'=4,'freq'=8] {'freq'}, dimensions={0} | all-to-all | bytes 1048576 | tf_op jit(solution)/shard_map/all_to_all | solution.py:177
  82.0 0.1 copy.32
  82.1 10.4 %all_to_all.26 = f32[4,16,2,1,128]{4,2,1,3,0:T(2,128)S(1)} all-to-all(f32[4,16,2,1,128]{4,2,1,3,0:T(2,128)S(1)} %copy.32), channel_id=1, replica_groups=mesh['grp'=4,'freq'=8] {'grp'}, dimensions={0} | all-to-all | bytes 131072 | tf_op jit(solution)/shard_map/all_to_all | solution.py:180
  92.5 0.1 reshape.29
  92.6 0.7 copy.34
  (8 shorter events, 0.1 us)
Async XLA Ops:
  0.0 8.6 %copy-start = (f32[3,8192]{1,0:T(4,128)S(1)}, f32[3,8192]{1,0:T(4,128)}, u32[]{:S(2)}) copy-start(f32[3,8192]{1,0:T(4,128)} %param.7) | copy-start | bytes 294916
  3.2 7.7 %copy-start.2 = (f32[3,2048]{1,0:T(4,128)S(1)}, f32[3,2048]{1,0:T(4,128)}, u32[]{:S(2)}) copy-start(f32[3,2048]{1,0:T(4,128)} %param.9) | copy-start | bytes 73732
  3.2 8.0 %copy-start.3 = (s32[32]{0:T(128)S(1)}, s32[32]{0:T(128)}, u32[]{:S(2)}) copy-start(s32[32]{0:T(128)} %param.10) | copy-start | bytes 388
  3.2 31.9 %all-to-all-start = ((bf16[128,8,1024]{2,0,1:T(8,128)(2,1)}), bf16[128,8,1024]{2,0,1:T(8,128)(2,1)S(1)}, u32[]{:S(2)}, u32[]{:S(2)}) async-start(bf16[128,8,1024]{2,0,1:T(8,128)(2,1)} %bitcast.22), calls=%async_computation | async-start | bytes 4194304 | tf_op jit(solution)/shard_map/all_to_all | solution.py:161
  35.2 1.3 %copy-start.1 = (bf16[128,8,1024]{2,0,1:T(8,128)(2,1)}, bf16[128,8,1024]{2,0,1:T(8,128)(2,1)S(1)}, u32[]{:S(2)}) copy-start(bf16[128,8,1024]{2,0,1:T(8,128)(2,1)S(1)} %all-to-all-done) | copy-start | bytes 6291460

commit v2 on v1

--- a/solution.py
+++ b/solution.py
@@ -13,6 +13,7 @@
 NF = 512
 NCOMP = 4
 WAVE_STEP = 0.04
+MESH = pl.DeviceIdType.MESH
 LANES = 128
 CHUNK = 256
 STEPS = 8
@@ -110,7 +111,7 @@
                 green_rows(states, later, k * per + r)
 
 
-def phase(q, first, table_ref, block_of, pos_ref, blade_ref, obs_ref, acc, spec, states, mask, ga, gb, share):
+def phase(q, first, table_ref, block_of, pos_ref, blade_ref, obs_ref, acc, spec, states, mask, ga, gb, share, done):
     row0 = pl.multiple_of(q * CHUNK, CHUNK)
     start_states(pos_ref, obs_ref, states, row0, share)
     sub = lax.broadcasted_iota(jnp.int32, (2 * NCOMP, CHUNK), 0) % NCOMP
@@ -130,22 +131,123 @@
     def two(i, carry):
         block_pair(spec, m, ga, acc, 2 * i, share, first, states, gb)
         block_pair(spec, m, gb, acc, 2 * i + 1, share, first, states, ga)
+        done(q, i)
         return carry
 
     lax.fori_loop(0, blocks // 2, two, 0)
 
 
-def kernel(share, table_ref, data_ref, pos_ref, blade_ref, obs_ref, acc, spec, states, mask, ga, gb):
+def kernel(share, size, table_ref, src_ref, pos_ref, blade_ref, obs_ref, out_ref, *scratch):
+    (acc, spec, states, mask, ga, gb, data, parts, total, zsend, zrecv) = scratch[:11]
+    (send_sem, recv_sem, part_send, part_recv, z_send, z_recv) = scratch[11:]
+    nfreq, ngrp = size
+    me, grp = lax.axis_index("freq"), lax.axis_index("grp")
+    rows = src_ref.shape[0]
+    panels = src_ref.shape[1] // nfreq
+    chunks = panels // CHUNK
+    mine = NF // share // nfreq
+
+    def freq_peer(d):
+        return lax.rem(me + d, nfreq)
+
+    barrier = pltpu.get_barrier_semaphore()
+
+    def greet(d, carry):
+        pl.semaphore_signal(barrier, inc=1, device_id={"freq": freq_peer(d)}, device_id_type=MESH)
+        return carry
+
+    lax.fori_loop(1, nfreq, greet, 0)
+    for d in range(1, ngrp):
+        pl.semaphore_signal(barrier, inc=1, device_id={"grp": lax.rem(grp + d, ngrp)}, device_id_type=MESH)
+    pl.semaphore_wait(barrier, nfreq + ngrp - 2)
+
+    def columns(owner, q):
+        return pl.ds(pl.multiple_of(owner * panels + q * CHUNK, CHUNK), CHUNK)
+
+    landing = pl.ds(pl.multiple_of(me * rows, rows), rows)
+
+    def send_chunk(q, carry):
+        def to(d, carry):
+            dest = freq_peer(d)
+            pltpu.make_async_remote_copy(
+                src_ref=src_ref.at[:, columns(dest, q)],
+                dst_ref=data.at[q, landing, :],
+                send_sem=send_sem.at[q],
+                recv_sem=recv_sem.at[q],
+                device_id={"freq": dest},
+                device_id_type=MESH,
+            ).start()
+            return carry
+
+        lax.fori_loop(1, nfreq, to, 0)
+        pltpu.make_async_copy(src_ref.at[:, columns(me, q)], data.at[q, landing, :], recv_sem.at[q]).start()
+        return carry
+
+    lax.fori_loop(0, chunks, send_chunk, 0)
+    acc[...] = jnp.zeros_like(acc)
+
     def block_of(q):
-        return data_ref[:, pl.ds(pl.multiple_of(q * CHUNK, CHUNK), CHUNK)]
-
-    acc[...] = jnp.zeros_like(acc)
+        pltpu.make_async_copy(data.at[q], data.at[q], recv_sem.at[q]).wait()
+        return data[q]
+
+    def done(q, i):
+        ranges = 2 * STEPS // mine
+
+        @pl.when(q == chunks - 1)
+        def _():
+            for r in range(ranges):
+                dest = i * ranges + r
+
+                @pl.when(dest != me)
+                def _():
+                    pltpu.make_async_remote_copy(
+                        src_ref=acc.at[pl.ds(dest * mine, mine)],
+                        dst_ref=parts.at[me],
+                        send_sem=part_send,
+                        recv_sem=part_recv,
+                        device_id={"freq": dest},
+                        device_id_type=MESH,
+                    ).start()
 
     def step(q, carry):
-        phase(q, False, table_ref, block_of, pos_ref, blade_ref, obs_ref, acc, spec, states, mask, ga, gb, share)
-        return carry
-
-    lax.fori_loop(0, data_ref.shape[1] // CHUNK, step, 0)
+        phase(q, False, table_ref, block_of, pos_ref, blade_ref, obs_ref, acc, spec, states, mask, ga, gb, share, done)
+        return carry
+
+    lax.fori_loop(0, chunks, step, 0)
+
+    parts[me] = acc[pl.ds(me * mine, mine)]
+    others = parts.at[pl.ds(0, nfreq - 1)]
+    pltpu.make_async_copy(others, others, part_recv).wait()
+    total[...] = jnp.sum(parts[...], axis=0)
+    held = NCOMP // ngrp
+    for g in range(ngrp):
+        for b in range(held):
+            for c in range(2):
+                at = (b * 2 + c) * mine
+                zsend[g, at : at + mine, :] = total[:, c * NCOMP + g * held + b, :]
+    for d in range(1, ngrp):
+        dest = lax.rem(grp + d, ngrp)
+        pltpu.make_async_remote_copy(
+            src_ref=zsend.at[dest],
+            dst_ref=zrecv.at[grp],
+            send_sem=z_send,
+            recv_sem=z_recv,
+            device_id={"grp": dest},
+            device_id_type=MESH,
+        ).start()
+    zrecv[grp] = zsend[grp]
+    rest = zrecv.at[pl.ds(0, ngrp - 1)]
+    pltpu.make_async_copy(rest, rest, z_recv).wait()
+    out_ref[...] = jnp.sum(zrecv[...], axis=0)
+    pltpu.make_async_copy(rest, rest, z_send).wait()
+    pltpu.make_async_copy(others, others, part_send).wait()
+
+    def drain(q, carry):
+        sent = data.at[q, pl.ds(0, (nfreq - 1) * rows), :]
+        pltpu.make_async_copy(sent, sent, send_sem.at[q]).wait()
+        return carry
+
+    lax.fori_loop(0, chunks, drain, 0)
 
 
 def body(sources, panel_pos, panel_blade, observer_table, observer_index):
@@ -154,32 +256,42 @@
     nobs = observer_index.shape[0]
     share = LANES // nobs
     panels = sources.shape[1] // nfreq
+    chunks = panels // CHUNK
     observers = jnp.tile(observer_table[:, observer_index], (1, share))
     pos = lax.dynamic_slice_in_dim(panel_pos, me * panels, panels, 1).T
     blade = lax.dynamic_slice_in_dim(panel_blade, me * panels, panels, 0)[None, :]
-    shaped = sources.reshape(sources.shape[0], nfreq, panels)
-    piece = lax.all_to_all(shaped, "freq", split_axis=1, concat_axis=0, tiled=True).reshape(NT, panels)
     steps = NF // share
-    partial = pl.pallas_call(
-        functools.partial(kernel, share),
-        out_shape=jax.ShapeDtypeStruct((steps, 2 * NCOMP, LANES), jnp.float32),
-        in_specs=[pl.BlockSpec(memory_space=pltpu.VMEM)] * 5,
-        out_specs=pl.BlockSpec(memory_space=pltpu.VMEM),
+    mine = steps // nfreq
+    held = NCOMP // ngrp
+    vmem = pl.BlockSpec(memory_space=pltpu.VMEM)
+    got = pl.pallas_call(
+        functools.partial(kernel, share, (nfreq, ngrp)),
+        out_shape=jax.ShapeDtypeStruct((2 * held * mine, LANES), jnp.float32),
+        in_specs=[vmem, pl.BlockSpec(memory_space=pl.ANY), vmem, vmem, vmem],
+        out_specs=vmem,
         scratch_shapes=[
+            pltpu.VMEM((steps, 2 * NCOMP, LANES), jnp.float32),
             pltpu.VMEM((2 * NF, CHUNK), jnp.float32),
             pltpu.VMEM((5, CHUNK, LANES), jnp.float32),
             pltpu.VMEM((2 * NCOMP, CHUNK), jnp.float32),
             pltpu.VMEM((STEPS, CHUNK, 2 * LANES), jnp.bfloat16),
             pltpu.VMEM((STEPS, CHUNK, 2 * LANES), jnp.bfloat16),
+            pltpu.VMEM((chunks, NT, CHUNK), jnp.bfloat16),
+            pltpu.VMEM((nfreq, mine, 2 * NCOMP, LANES), jnp.float32),
+            pltpu.VMEM((mine, 2 * NCOMP, LANES), jnp.float32),
+            pltpu.VMEM((ngrp, 2 * held * mine, LANES), jnp.float32),
+            pltpu.VMEM((ngrp, 2 * held * mine, LANES), jnp.float32),
+            pltpu.SemaphoreType.DMA((chunks,)),
+            pltpu.SemaphoreType.DMA((chunks,)),
+            pltpu.SemaphoreType.DMA,
+            pltpu.SemaphoreType.DMA,
+            pltpu.SemaphoreType.DMA,
+            pltpu.SemaphoreType.DMA,
         ],
-    )(transform_table(), piece, pos, blade, observers)
-    mine = steps // nfreq
-    parts = lax.all_to_all(partial.reshape(nfreq, mine, 2 * NCOMP, LANES), "freq", split_axis=0, concat_axis=0, tiled=True)
-    summed = jnp.sum(parts, axis=0)
-    blades = summed.reshape(mine, 2, ngrp, NCOMP // ngrp, LANES).transpose(2, 0, 1, 3, 4)
-    got = jnp.sum(lax.all_to_all(blades, "grp", split_axis=0, concat_axis=0, tiled=True), axis=0)
-    got = got.reshape(mine, 2, NCOMP // ngrp, share, nobs).transpose(0, 3, 2, 1, 4)
-    return got.reshape(mine * share, NCOMP // ngrp, 2, nobs)
+        compiler_params=pltpu.CompilerParams(collective_id=0, has_side_effects=True),
+    )(transform_table(), sources, pos, blade, observers)
+    got = got.reshape(held, 2, mine, share, nobs).transpose(2, 3, 0, 1, 4)
+    return got.reshape(mine * share, held, 2, nobs)
 
 
 def solution(mesh):

time: 93.8 us -> 59.4 us (0.63)
  the two profiles are of different devices: /device:TPU:0 before, /device:TPU:7 now
where the time goes in v2:
time: 59.4 us; the launch traced here: 59.1 us
  Pallas kernels  52.1 us (88%)
  local copies, waits for them, and re-layouts  6.25 us (11%)
  other arithmetic  0.7 us (1%)
    pallas_call x1, Pallas kernels, body(): pl.pallas_call(functools.partial(kernel, share, (nfreq, ngrp)), out_shape...  52.1 us
    unnamed x4, local copies, waits for them, and re-layouts  2.14 us
    dynamic_slice x1, local copies, waits for them, and re-layouts, body(): lax.dynamic_slice_in_dim(panel_blade, me * panels, panels, 0)[None, :]  1.28 us

profile of v2, /device:TPU:7, one launch (start us, length us, event | category | flops | bytes accessed | tf_op | source)
XLA Modules:
  0.0 59.1 jit_solution(13716465538121938873)
XLA Ops:
  0.0 0.0 copy-start
  0.0 0.7 %compare_select_fusion = s32[32]{0:T(128)S(1)} fusion(s32[32]{0:T(128)} %param.10), kind=kLoop, calls=%fused_computation.2 | loop fusion | flops 96 | bytes 256 | tf_op jit(solution)/shard_map/select_n | solution.py:260
  0.7 1.3 %dynamic_slice.7 = s32[1024]{0:T(1024)} dynamic-slice(s32[8192]{0:T(1024)} %param.8, s32[]{:T(128)S(6)} %select_n.7), dynamic_slice_sizes={1024} | dynamic-slice | bytes 8196 | tf_op jit(solution)/shard_map/dynamic_slice | solution.py:262
  2.0 0.0 copy-done
  2.0 1.0 %copy.15 = f32[3,1024]{0,1:T(8,128)} copy(f32[3,1024]{1,0:T(4,128)S(1)} %constant_dynamic-slice_fusion) | data formatting | bytes 24576
  3.0 1.1 %copy.12 = f32[3,2048]{0,1:T(8,128)S(1)} copy(f32[3,2048]{1,0:T(4,128)} %param.9) | data formatting | bytes 49152 | tf_op args[3]
  4.1 0.6 gather_fusion
  4.7 0.1 copy.13
  4.8 0.7 %tile.10.obs_ref = f32[3,128]{1,0:T(4,128)} reshape(f32[3,4,32]{2,1,0:T(4,128)S(1)} %tile.4) | data formatting | bytes 3072 | tf_op jit(solution)/shard_map/tile | solution.py:260
  5.5 52.1 %shard_map.64 = f32[32,128]{1,0:T(8,128)} custom-call(bf16[1024,1024]{1,0:T(8,128)(2,1)} %constant.16.table_ref, bf16[128,8192]{1,0:T(8,128)(2,1)} %src_ref.1, f32[1024,3]{1,0:T(8,128)} %bitcast.6, s32[1,1024]{1,0:T(1,128)} %bitcast.9, f32[3,128]{1,0:T(4,128)} %tile.10.obs_ref), custom_call_target="tpu_custom_call" | custom-call | tf_op jit(solution)/shard_map/pallas_call | solution.py:267
  57.6 0.8 %reshape.10 = f32[1,2,16,4,32]{4,3,2,1,0:T(4,128)S(1)} reshape(f32[32,128]{1,0:T(8,128)} %shard_map.64) | data formatting | bytes 32768 | tf_op jit(solution)/shard_map/reshape | solution.py:293
  58.4 0.7 %copy.14 = f32[64,1,2,32]{0,3,2,1:T(8,128)} copy(f32[64,1,2,32]{3,0,2,1:T(8,128)S(1)} %bitcast.7) | data formatting | bytes 32768 | tf_op jit(solution)/shard_map/reshape | solution.py:294
  (3 shorter events, 0.0 us)
Async XLA Ops:
  0.0 2.0 %copy-start = (f32[3,8192]{1,0:T(4,128)S(1)}, f32[3,8192]{1,0:T(4,128)}, u32[]{:S(2)}) copy-start(f32[3,8192]{1,0:T(4,128)} %param.7) | copy-start | bytes 294916

commit v3 on v2

--- a/solution.py
+++ b/solution.py
@@ -38,15 +38,15 @@
     return cos, sin * x
 
 
-def start_states(pos_ref, obs_ref, states, row0, share):
+def start_states(pos, obs, states, zero, share, turns, bits):
     rows = 32
     lane = lax.broadcasted_iota(jnp.int32, (rows, LANES), 1)
     j = (lane // (LANES // share)).astype(jnp.float32)
     for r in range(CHUNK // rows):
-        at = pl.ds(row0 + r * rows, rows)
+        at = slice(r * rows, (r + 1) * rows)
         d2 = None
         for axis in range(3):
-            diff = obs_ref[axis : axis + 1, :] - pos_ref[at, axis : axis + 1]
+            diff = obs[axis : axis + 1, :] - pos[at, axis : axis + 1]
             d2 = diff * diff if d2 is None else d2 + diff * diff
         d = jnp.sqrt(d2)
         amplitude = 0.25 / (math.pi * d)
@@ -54,12 +54,19 @@
         cj, sj = cos_sin(j * theta)
         cs, ss = cos_sin(float(share) * theta)
         cj, sj = cj * amplitude, sj * amplitude
-        out = pl.ds(r * rows, rows)
-        states[0, out, :] = cj * cs + sj * ss
-        states[1, out, :] = cj
-        states[2, out, :] = sj * cs - cj * ss
-        states[3, out, :] = sj
-        states[4, out, :] = 2.0 * cs
+        c0, s0 = cj * cs + sj * ss, sj * cs - cj * ss
+        zero[0, at, :], zero[1, at, :], zero[2, at, :], zero[3, at, :] = c0, cj, s0, sj
+        states[4, at, :] = 2.0 * cs
+        for _ in range((2 * STEPS).bit_length() - 1):
+            cs, ss = cs * cs - ss * ss, 2.0 * cs * ss
+        for b in range(bits):
+            keep = lax.rem(lax.div(turns, 2**b), 2) == 1
+            ct, st = jnp.where(keep, cs, 1.0), jnp.where(keep, ss, 0.0)
+            c0, s0 = c0 * ct - s0 * st, s0 * ct + c0 * st
+            cj, sj = cj * ct - sj * st, sj * ct + cj * st
+            if b < bits - 1:
+                cs, ss = cs * cs - ss * ss, 2.0 * cs * ss
+        states[0, at, :], states[1, at, :], states[2, at, :], states[3, at, :] = c0, cj, s0, sj
 
 
 def green_rows(states, green, r):
@@ -111,12 +118,10 @@
                 green_rows(states, later, k * per + r)
 
 
-def phase(q, first, table_ref, block_of, pos_ref, blade_ref, obs_ref, acc, spec, states, mask, ga, gb, share, done):
-    row0 = pl.multiple_of(q * CHUNK, CHUNK)
-    start_states(pos_ref, obs_ref, states, row0, share)
+def phase(q, table_ref, block_of, blade, acc, spec, states, zero, mask, ga, gb, share, start, done):
     sub = lax.broadcasted_iota(jnp.int32, (2 * NCOMP, CHUNK), 0) % NCOMP
-    mask[...] = jnp.where(blade_ref[:, pl.ds(row0, CHUNK)] == sub, 1.0, 0.0)
-    block_pair(None, None, None, None, 0, share, first, states, ga)
+    mask[...] = jnp.where(blade == sub, 1.0, 0.0)
+    block_pair(None, None, None, None, 0, share, False, states, ga)
     data = block_of(q)
     for r in range(4):
         part = pl.ds(r * (2 * NF // 4), 2 * NF // 4)
@@ -125,21 +130,27 @@
             .astype(jnp.bfloat16)
             .astype(jnp.float32)
         )
-    blocks = NF // share // STEPS
-    m = mask[...]
+    pairs = NF // share // STEPS // 2
 
     def two(i, carry):
-        block_pair(spec, m, ga, acc, 2 * i, share, first, states, gb)
-        block_pair(spec, m, gb, acc, 2 * i + 1, share, first, states, ga)
-        done(q, i)
-        return carry
-
-    lax.fori_loop(0, blocks // 2, two, 0)
-
-
-def kernel(share, size, table_ref, src_ref, pos_ref, blade_ref, obs_ref, out_ref, *scratch):
-    (acc, spec, states, mask, ga, gb, data, parts, total, zsend, zrecv) = scratch[:11]
-    (send_sem, recv_sem, part_send, part_recv, z_send, z_recv) = scratch[11:]
+        m = mask[...]
+        at = lax.rem(start + i, pairs)
+        block_pair(spec, m, ga, acc, 2 * at, share, False, states, gb)
+
+        @pl.when(at == pairs - 1)
+        def _():
+            states[0:4] = zero[...]
+
+        block_pair(spec, m, gb, acc, 2 * at + 1, share, False, states, ga)
+        done(q, at)
+        return carry
+
+    lax.fori_loop(0, pairs, two, 0)
+
+
+def kernel(share, size, table_ref, src_ref, pos_ref, blade_ref, obs_ref, index_ref, out_ref, *scratch):
+    (acc, spec, states, zero, mask, ga, gb, data, parts, total, zsend, zrecv, tail) = scratch[:13]
+    (send_sem, recv_sem, part_send, part_recv, z_send, z_recv) = scratch[13:]
     nfreq, ngrp = size
     me, grp = lax.axis_index("freq"), lax.axis_index("grp")
     rows = src_ref.shape[0]
@@ -185,6 +196,21 @@
 
     lax.fori_loop(0, chunks, send_chunk, 0)
     acc[...] = jnp.zeros_like(acc)
+    pairs = NF // share // STEPS // 2
+    start = lax.rem(lax.div(me * mine, 2 * STEPS) + 1, pairs)
+    index = jnp.concatenate([index_ref[...]] * share, axis=1)
+    entry = lax.broadcasted_iota(jnp.int32, (obs_ref.shape[1], LANES), 0)
+    chosen = jnp.where(entry == index, 1.0, 0.0)
+    obs = jnp.dot(
+        obs_ref[...], chosen, preferred_element_type=jnp.float32, precision=lax.Precision.HIGHEST
+    )
+
+    def prepare(q, carry):
+        pos = jnp.concatenate([pos_ref[:, columns(me, q)], jnp.zeros((5, CHUNK), jnp.float32)], axis=0)
+        start_states(pos.T, obs, states.at[q], zero.at[q], share, start, pairs.bit_length() - 1)
+        return carry
+
+    lax.fori_loop(0, chunks, prepare, 0)
 
     def block_of(q):
         pltpu.make_async_copy(data.at[q], data.at[q], recv_sem.at[q]).wait()
@@ -210,7 +236,7 @@
                     ).start()
 
     def step(q, carry):
-        phase(q, False, table_ref, block_of, pos_ref, blade_ref, obs_ref, acc, spec, states, mask, ga, gb, share, done)
+        phase(q, table_ref, block_of, blade_ref[:, columns(me, q)], acc, spec, states.at[q], zero.at[q], mask, ga, gb, share, start, done)
         return carry
 
     lax.fori_loop(0, chunks, step, 0)
@@ -238,7 +264,16 @@
     zrecv[grp] = zsend[grp]
     rest = zrecv.at[pl.ds(0, ngrp - 1)]
     pltpu.make_async_copy(rest, rest, z_recv).wait()
-    out_ref[...] = jnp.sum(zrecv[...], axis=0)
+    final = jnp.sum(zrecv[...], axis=0)
+    nobs = LANES // share
+    for j in range(share):
+        tail[j] = final[:, j * nobs : (j + 1) * nobs]
+    for t in range(mine):
+        for j in range(share):
+            for b in range(held):
+                for c in range(2):
+                    row = (b * 2 + c) * mine + t
+                    out_ref[t * share + j, b, c : c + 1, :] = tail[j, row : row + 1, :]
     pltpu.make_async_copy(rest, rest, z_send).wait()
     pltpu.make_async_copy(others, others, part_send).wait()
 
@@ -252,35 +287,34 @@
 
 def body(sources, panel_pos, panel_blade, observer_table, observer_index):
     nfreq, ngrp = lax.axis_size("freq"), lax.axis_size("grp")
-    me = lax.axis_index("freq")
     nobs = observer_index.shape[0]
     share = LANES // nobs
     panels = sources.shape[1] // nfreq
     chunks = panels // CHUNK
-    observers = jnp.tile(observer_table[:, observer_index], (1, share))
-    pos = lax.dynamic_slice_in_dim(panel_pos, me * panels, panels, 1).T
-    blade = lax.dynamic_slice_in_dim(panel_blade, me * panels, panels, 0)[None, :]
     steps = NF // share
     mine = steps // nfreq
     held = NCOMP // ngrp
     vmem = pl.BlockSpec(memory_space=pltpu.VMEM)
-    got = pl.pallas_call(
+    f32 = jnp.float32
+    return pl.pallas_call(
         functools.partial(kernel, share, (nfreq, ngrp)),
-        out_shape=jax.ShapeDtypeStruct((2 * held * mine, LANES), jnp.float32),
-        in_specs=[vmem, pl.BlockSpec(memory_space=pl.ANY), vmem, vmem, vmem],
+        out_shape=jax.ShapeDtypeStruct((NF // nfreq, held, 2, nobs), f32),
+        in_specs=[vmem, pl.BlockSpec(memory_space=pl.ANY)] + [vmem] * 4,
         out_specs=vmem,
         scratch_shapes=[
-            pltpu.VMEM((steps, 2 * NCOMP, LANES), jnp.float32),
-            pltpu.VMEM((2 * NF, CHUNK), jnp.float32),
-            pltpu.VMEM((5, CHUNK, LANES), jnp.float32),
-            pltpu.VMEM((2 * NCOMP, CHUNK), jnp.float32),
+            pltpu.VMEM((steps, 2 * NCOMP, LANES), f32),
+            pltpu.VMEM((2 * NF, CHUNK), f32),
+            pltpu.VMEM((chunks, 5, CHUNK, LANES), f32),
+            pltpu.VMEM((chunks, 4, CHUNK, LANES), f32),
+            pltpu.VMEM((2 * NCOMP, CHUNK), f32),
             pltpu.VMEM((STEPS, CHUNK, 2 * LANES), jnp.bfloat16),
             pltpu.VMEM((STEPS, CHUNK, 2 * LANES), jnp.bfloat16),
             pltpu.VMEM((chunks, NT, CHUNK), jnp.bfloat16),
-            pltpu.VMEM((nfreq, mine, 2 * NCOMP, LANES), jnp.float32),
-            pltpu.VMEM((mine, 2 * NCOMP, LANES), jnp.float32),
-            pltpu.VMEM((ngrp, 2 * held * mine, LANES), jnp.float32),
-            pltpu.VMEM((ngrp, 2 * held * mine, LANES), jnp.float32),
+            pltpu.VMEM((nfreq, mine, 2 * NCOMP, LANES), f32),
+            pltpu.VMEM((mine, 2 * NCOMP, LANES), f32),
+            pltpu.VMEM((ngrp, 2 * held * mine, LANES), f32),
+            pltpu.VMEM((ngrp, 2 * held * mine, LANES), f32),
+            pltpu.VMEM((share, 2 * held * mine, nobs), f32),
             pltpu.SemaphoreType.DMA((chunks,)),
             pltpu.SemaphoreType.DMA((chunks,)),
             pltpu.SemaphoreType.DMA,
@@ -289,9 +323,7 @@
             pltpu.SemaphoreType.DMA,
         ],
         compiler_params=pltpu.CompilerParams(collective_id=0, has_side_effects=True),
-    )(transform_table(), sources, pos, blade, observers)
-    got = got.reshape(held, 2, mine, share, nobs).transpose(2, 3, 0, 1, 4)
-    return got.reshape(mine * share, held, 2, nobs)
+    )(transform_table(), sources, panel_pos, panel_blade[None, :], observer_table, observer_index[None, :])
 
 
 def solution(mesh):

time: 59.4 us -> 51.2 us (0.86)
  the two profiles are of different devices: /device:TPU:7 before, /device:TPU:0 now
where the time goes in v3:
time: 51.2 us; the launch traced here: 51 us
  Pallas kernels  49.5 us (97%)
  local copies, waits for them, and re-layouts  1.53 us (3%)
    pallas_call x1, Pallas kernels, body(): pl.pallas_call(functools.partial(kernel, share, (nfreq, ngrp)), out_shape...  49.5 us
    pallas_call x1, local copies, waits for them, and re-layouts, body(): pl.pallas_call(functools.partial(kernel, share, (nfreq, ngrp)), out_shape...  1.53 us

profile of v3, /device:TPU:0, one launch (start us, length us, event | category | flops | bytes accessed | tf_op | source)
XLA Modules:
  0.0 51.0 jit_solution(7847800565697412831)
XLA Ops:
  0.0 49.5 %shard_map.64 = f32[64,1,2,32]{3,2,1,0:T(2,128)} custom-call(bf16[1024,1024]{1,0:T(8,128)(2,1)} %constant.3.table_ref, bf16[128,8192]{1,0:T(8,128)(2,1)} %src_ref.1, f32[3,8192]{1,0:T(4,128)} %pos_ref.1, s32[1,8192]{1,0:T(1,128)} %bitcast.2, f32[3,2048]{1,0:T(4,128)} %obs_ref.1, s32[1,32]{1,0:T(1,128)} %bitcast.3), custom_call_target="tpu_custom_call" | custom-call | tf_op jit(solution)/shard_map/pallas_call | solution.py:299
  49.5 1.5 %copy.7 = f32[64,1,2,32]{0,3,2,1:T(8,128)} copy(f32[64,1,2,32]{3,2,1,0:T(2,128)} %shard_map.64) | data formatting | bytes 32768 | tf_op jit(solution)/shard_map/pallas_call | solution.py:299

commit v4 on v3

--- a/solution.py
+++ b/solution.py
@@ -141,7 +141,10 @@
         def _():
             states[0:4] = zero[...]
 
-        block_pair(spec, m, gb, acc, 2 * at + 1, share, False, states, ga)
+        @pl.when(at < pairs)
+        def _():
+            block_pair(spec, mask[...], gb, acc, 2 * at + 1, share, False, states, ga)
+
         done(q, at)
         return carry
 

time: 51.2 us -> 49.4 us (0.965)
  Pallas kernels: 49.5 us -> 47.7 us
    pallas_call x1, Pallas kernels: 49.5 us -> 47.7 us  [body(): pl.pallas_call(functools.partial(kernel, share, (nfreq, ngrp)), out_shape...]
where the time goes in v4:
time: 49.4 us; the launch traced here: 49.2 us
  Pallas kernels  47.7 us (97%)
  local copies, waits for them, and re-layouts  1.53 us (3%)
    pallas_call x1, Pallas kernels, body(): pl.pallas_call(functools.partial(kernel, share, (nfreq, ngrp)), out_shape...  47.7 us
    pallas_call x1, local copies, waits for them, and re-layouts, body(): pl.pallas_call(functools.partial(kernel, share, (nfreq, ngrp)), out_shape...  1.53 us

profile of v4, /device:TPU:0, one launch (start us, length us, event | category | flops | bytes accessed | tf_op | source)
XLA Modules:
  0.0 49.2 jit_solution(6851608843967401804)
XLA Ops:
  0.0 47.7 %shard_map.64 = f32[64,1,2,32]{3,2,1,0:T(2,128)} custom-call(bf16[1024,1024]{1,0:T(8,128)(2,1)} %constant.3.table_ref, bf16[128,8192]{1,0:T(8,128)(2,1)} %src_ref.1, f32[3,8192]{1,0:T(4,128)} %pos_ref.1, s32[1,8192]{1,0:T(1,128)} %bitcast.2, f32[3,2048]{1,0:T(4,128)} %obs_ref.1, s32[1,32]{1,0:T(1,128)} %bitcast.3), custom_call_target="tpu_custom_call" | custom-call | tf_op jit(solution)/shard_map/pallas_call | solution.py:302
  47.7 1.5 %copy.7 = f32[64,1,2,32]{0,3,2,1:T(8,128)} copy(f32[64,1,2,32]{3,2,1,0:T(2,128)} %shard_map.64) | data formatting | bytes 32768 | tf_op jit(solution)/shard_map/pallas_call | solution.py:302
